TPU v7x, 256 devices: a whole 4x4x8 slice. The times are simulated.
256 devices in a mesh: swath: 8 (over y_hi, x), bulk: 32 (over y_lo, z, core).
Axes of the slice: x: 4, y: 4 (y_hi: 2, y_lo: 2; y = y_hi * 2 + y_lo), z: 8, core: 2. Of those that a mesh axis runs over, the one named last changes fastest.
Arguments:
- image: float32 [32, 2048, 1024], P('bulk', None, 'swath'), may hold values from -6 to 6
- offsets: int32 [32], P('bulk'), may hold values from -128 to 127
Outputs:
- defect: float32 [32, 2048, 1024], P('bulk', None, 'swath')
All inputs are finite; a program needn't handle non-finite values.
Results may differ from a plain program's by a relative error of at most 0.00025.
Values sent between devices are 32-bit elements; how exact they have to be, the bound alone decides.
No kernel may reach another device: no remote copies, remote signals or barrier semaphores. Data moves between devices by JAX's collectives and lax.ppermute only.
A program may use at most 64 MiB of HBM per device.

v0:
```python
import functools
import math

import jax
import jax.numpy as jnp
from jax import lax
from jax.experimental import pallas as pl
from jax.experimental.pallas import tpu as pltpu
from jax.sharding import PartitionSpec as P

DIE_SPAN = 4
COLS = 2048
LANES = 128
HALO = 32
ROWS_A = 1344
ROWS_B = COLS - ROWS_A
KEEP_A = ROWS_A - 32
WINDOW = 192
WINDOWS_A = -(-KEEP_A // WINDOW)
WINDOWS_B = -(-(COLS - KEEP_A) // WINDOW)
START_B = COLS - WINDOWS_B * WINDOW - HALO
OLD_B = ROWS_A - START_B

F32 = jnp.float32
BF16 = jnp.bfloat16
VMEM = pl.BlockSpec(memory_space=pltpu.VMEM)
SMEM = pl.BlockSpec(memory_space=pltpu.SMEM)
ANY = pl.BlockSpec(memory_space=pl.ANY)
PARAMS = pltpu.CompilerParams(vmem_limit_bytes=40 << 20)


def split(value):
    high = value.astype(BF16)
    return high, (value - high.astype(F32)).astype(BF16)


def tables_kernel(flags, row_high, row_low, col_high, col_low):
    shape = (256, 256)
    down = lax.broadcasted_iota(jnp.int32, shape, 0)
    across = lax.broadcasted_iota(jnp.int32, shape, 1)
    apart = (down - across) & 255
    apart = jnp.minimum(apart, 256 - apart)
    blurs = []
    for octave in range(4):
        reach = 2**octave
        weight = jnp.where(apart == 0, 6.0, jnp.where(apart == reach, 4.0, jnp.where(apart == 2 * reach, 1.0, 0.0)))
        blurs.append(weight.astype(BF16))
    inside = (across < LANES).astype(jnp.int32)
    inside = inside + ((across >= LANES) & (across < LANES + HALO)).astype(jnp.int32) * flags[3]
    inside = (inside + (across >= 256 - HALO).astype(jnp.int32) * flags[2]).astype(F32)
    total = jnp.where(down == across, inside, 0.0)
    for octave in range(4):
        high, low = split(total)
        total = inside * (
            jnp.dot(high, blurs[octave], preferred_element_type=F32)
            + jnp.dot(low, blurs[octave], preferred_element_type=F32)
        )
        high, low = split(total[:, :LANES] * 256.0 ** -(octave + 1))
        row_high[:, octave * LANES : (octave + 1) * LANES] = high
        if octave >= 2:
            row_low[:, (octave - 2) * LANES : (octave - 1) * LANES] = low
    for case, inside in enumerate((down >= HALO, down >= 0, down < 256 - HALO)):
        inside = inside.astype(F32)
        total = jnp.where(down == across, inside, 0.0)
        for octave in range(4):
            high, low = split(total)
            total = inside * (
                jnp.dot(blurs[octave], high, preferred_element_type=F32)
                + jnp.dot(blurs[octave], low, preferred_element_type=F32)
            )
            high, low = split(total[HALO : 256 - HALO])
            col_high[case, octave] = high
            if octave >= 2:
                col_low[case, octave - 2] = low


def lanes(shape):
    return lax.broadcasted_iota(jnp.int32, shape, 1)


def signs(shape):
    return (1 - 2 * (lax.broadcasted_iota(jnp.int32, shape, 0) % 2)).astype(F32)


def sine(x):
    y = x * x
    total = jnp.full_like(x, 1 / math.factorial(13))
    for power in (11, 9, 7, 5, 3, 1):
        total = total * y + (-1) ** ((power - 1) // 2) / math.factorial(power)
    return total * x


def cosine(x):
    y = x * x
    total = jnp.full_like(x, -1 / math.factorial(14))
    for power in (12, 10, 8, 6, 4, 2, 0):
        total = total * y + (-1) ** (power // 2) / math.factorial(power)
    return total


def turned_sine(moves):
    turns = jnp.floor(moves * (1 / 64) + 0.5)
    parity = turns - 2 * jnp.floor(turns * 0.5)
    return (1 - 2 * parity) * sine((moves - 64 * turns) * (math.pi / 64))


def nyquist(v):
    folded = v.reshape(COLS // 8, 8, LANES).sum(axis=0)
    return jnp.sum(folded * signs((8, LANES)), axis=0, keepdims=True) * (1 / COLS)


def pack(v, out_left, out_right, at):
    n = v.shape[0] // 4
    lane = lanes((n, LANES))
    left = right = None
    for q in range(4):
        piece = v[q * n : (q + 1) * n]
        here = (lane >= 32 * q) & (lane < 32 * q + 32)
        to_left = pltpu.roll(piece, 32 * q, 1) if q else piece
        to_right = pltpu.roll(piece, (32 * q + 32) % 128, 1) if q < 3 else piece
        left = to_left if left is None else jnp.where(here, to_left, left)
        right = to_right if right is None else jnp.where(here, to_right, right)
    out_left[at : at + n, :] = left
    out_right[at : at + n, :] = right


def unpack(from_right, from_left, q):
    lane = lanes(from_right.shape)
    right = pltpu.roll(from_right, (128 - 32 * q) % 128, 1) if q else from_right
    left = pltpu.roll(from_left, (96 - 32 * q) % 128, 1) if q < 3 else from_left
    return jnp.where(lane < HALO, right, jnp.where(lane >= LANES - HALO, left, 0.0))


def head_kernel(move, x, adn, aup, ny, pleft, pright):
    v = x[...]
    own = move[0].astype(F32)
    tone = nyquist(v)
    ny[...] = jnp.broadcast_to(tone, (8, LANES))
    wave = turned_sine(jnp.full((8, LANES), own, F32))
    swing = (wave * wave * jnp.broadcast_to(tone, (8, LANES)) * signs((8, LANES)))[None]
    adn[...] = v[:ROWS_A]
    first = v[:ROWS_A].reshape(ROWS_A // 8, 8, LANES) - swing
    aup[:ROWS_A, :] = first.reshape(ROWS_A, LANES)
    aup[ROWS_A:, :] = jnp.full((8, LANES), own, F32)
    pack(v, pleft, pright, 0)


def edge_kernel(move, x, ny, from_right, from_left, h, bdn, bup):
    n = COLS // 4
    for q in range(4):
        h[q * n : (q + 1) * n, :] = unpack(from_right[...], from_left[...], q)
    own = move[0].astype(F32)
    wave = turned_sine(jnp.full((8, LANES), own, F32))
    gain = wave * wave * signs((8, LANES))
    swing = (gain * ny[...])[None]
    hswing = (gain * jnp.broadcast_to(nyquist(h[...]), (8, LANES)))[None]
    half = ROWS_B // 2
    lane = lanes((half, LANES))

    def put(main, edge, out):
        out[:ROWS_B, :] = main
        one, two = edge[:half], edge[half:]
        out[ROWS_B:, :] = jnp.where(
            lane < 32,
            one,
            jnp.where(lane < 64, pltpu.roll(two, 32, 1), jnp.where(lane < 96, pltpu.roll(one, 96, 1), two)),
        )

    main = x[ROWS_A:, :]
    edge = h[ROWS_A:, :]
    put(main, edge, bdn)
    shape = (ROWS_B // 8, 8, LANES)
    put(
        (main.reshape(shape) - swing).reshape(ROWS_B, LANES),
        (edge.reshape(shape) - hswing).reshape(ROWS_B, LANES),
        bup,
    )


def shift_kernel(sign, move, x, h, out, hi, lo, ev, od):
    if sign > 0:
        moves = jnp.full((8, COLS), move[0].astype(F32), F32)
    else:
        moves = -jnp.concatenate([move[ROWS_A:, :]] * (COLS // LANES), axis=1)
    place = lax.broadcasted_iota(jnp.int32, (8, COLS), 1)
    delay = (1024 - place).astype(F32)
    steps = 64 * delay - moves
    turns = jnp.floor(steps * (1 / 65536) + 0.5)
    rest = steps - 65536 * turns
    flip = 1 - 2 * (turns - 2 * jnp.floor(turns * 0.5))
    theta = rest * (math.pi / 65536)
    hit = rest == 0.0
    parity = (1 - 2 * (place % 2)).astype(F32)
    base = parity * turned_sine(moves) * (-0.5 / 1024) / jnp.where(hit, 1.0, sine(theta))
    even = jnp.where(hit, 0.5, base * cosine(theta))
    odd = flip * jnp.where(hit, 0.5, base)
    for part, row in enumerate((even, odd)):
        slope = pltpu.roll(row, 0, 1, stride=1, stride_axis=0)
        for g in range(32):
            band = pltpu.roll(slope, 8 * g, 1) if g else slope
            top = band.astype(BF16)
            hi[part, 8 * g : 8 * g + 8, :] = top
            lo[part, 8 * g : 8 * g + 8, :] = (band - top.astype(F32)).astype(BF16)
    for at, ref in enumerate((x, h)):
        a = ref[:1024, :]
        b = ref[1024:, :]
        for held, value in ((ev, a + b), (od, a - b)):
            top = value.astype(BF16)
            held[0, :, at * LANES : (at + 1) * LANES] = top
            held[1, :, at * LANES : (at + 1) * LANES] = (value - top.astype(F32)).astype(BF16)
    for b in range(4):
        span = slice(1024 - 256 * b, 2048 - 256 * b)
        sums = []
        for part, held in ((0, ev), (1, od)):
            high = hi[part, :, span]
            low = lo[part, :, span]
            sums.append(
                jnp.dot(high, held[0], preferred_element_type=F32)
                + jnp.dot(high, held[1], preferred_element_type=F32)
                + jnp.dot(low, held[0], preferred_element_type=F32)
            )
        out[256 * b : 256 * b + 256, :] = sums[0] + sums[1]
        out[1024 + 256 * b : 1280 + 256 * b, :] = sums[0] - sums[1]


def pack_kernel(an, ap, xleft, xright):
    pack(an[...], xleft, xright, 0)
    pack(ap[:ROWS_A, :], xleft, xright, ROWS_A // 4)


def score_stage(count, cases, blocks, flags, row_high, row_low, col_high, col_low, d, yh, yl, out, sem, keep, base):
    length = count * WINDOW + 64
    filled = []
    for start, rows, make in blocks:
        filled.append((start, start + rows))
        am, ah, bm, bh = make()
        has_ahead = flags[0] > 0
        has_behind = flags[1] > 0
        pairs = (
            (jnp.where(has_ahead, am, bm), jnp.where(has_ahead, ah, bh)),
            (jnp.where(has_behind, bm, am), jnp.where(has_behind, bh, ah)),
        )
        here = slice(start, start + rows)
        for which, (main, edge) in enumerate(pairs):
            side = slice(which * LANES, (which + 1) * LANES)
            d[here, side] = main
            high, low = split(jnp.concatenate([main, edge], axis=1))
            for tile in range(2):
                part = slice(256 * tile, 256 * tile + 256)
                y = jnp.dot(high, row_high[:, part], preferred_element_type=F32)
                y = y + jnp.dot(low, row_high[:, part], preferred_element_type=F32)
                if tile:
                    y = y + jnp.dot(high, row_low[...], preferred_element_type=F32)
                top, rest = split(y)
                for k in range(2):
                    yh[2 * tile + k, here, side] = top[:, k * LANES : (k + 1) * LANES]
                    yl[2 * tile + k, here, side] = rest[:, k * LANES : (k + 1) * LANES]
    gaps = [(filled[i][1], filled[i + 1][0]) for i in range(len(filled) - 1)]
    for low, high in [(0, filled[0][0])] + gaps + [(filled[-1][1], length)]:
        if low < high:
            for k in range(4):
                yh[k, low:high, :] = jnp.zeros((high - low, 256), BF16)
                yl[k, low:high, :] = jnp.zeros((high - low, 256), BF16)
    copies = []
    for w in range(count):
        case = cases[0] if w == 0 else cases[2] if w == count - 1 else cases[1]
        span = slice(WINDOW * w, WINDOW * w + 256)
        before = d[HALO + WINDOW * w : HALO + WINDOW * (w + 1), :]
        score = None
        for k in range(4):
            after = jnp.dot(col_high[case, k], yh[k, span, :], preferred_element_type=F32)
            after = after + jnp.dot(col_high[case, k], yl[k, span, :], preferred_element_type=F32)
            if k >= 2:
                after = after + jnp.dot(col_low[case, k - 2], yh[k, span, :], preferred_element_type=F32)
            gap = before - after
            score = gap * gap if score is None else score + 2.0**k * (gap * gap)
            before = after
        d[HALO + WINDOW * w : HALO + WINDOW * (w + 1), :LANES] = score[:, :LANES] * score[:, LANES:]
    low, high = keep
    copy = pltpu.make_async_copy(
        d.at[pl.ds(HALO + low, high - low), pl.ds(0, LANES)], out.at[pl.ds(base + low, high - low)], sem
    )
    copy.start()
    copy.wait()


def first_kernel(flags, sa, sb, an, ap, gright, gleft, rh, rl, ch, cl, out, d, yh, yl, sem):
    n = ROWS_A // 4

    def block(q):
        def make():
            here = slice(q * n, q * n + n)
            parts = []
            for which, (own, other) in enumerate(((sa, an), (sb, ap))):
                edge = unpack(gright[which * n : which * n + n, :], gleft[which * n : which * n + n, :], q)
                parts += [own[here, :LANES] - other[here, :], own[here, LANES:] - edge]
            return parts

        return (HALO + q * n, n, make)

    score_stage(
        WINDOWS_A, (0, 1, 1), [block(q) for q in range(4)], flags, rh, rl, ch, cl, d, yh, yl, out, sem, (0, KEEP_A), 0
    )


def second_kernel(flags, sa, sb, an, ap, gright, gleft, bn, bp, rh, rl, ch, cl, _, out, d, yh, yl, sem):
    n = ROWS_A // 4
    half = ROWS_B // 2
    lane = lanes((half, LANES))

    def old():
        parts = []
        for which, (own, other) in enumerate(((sa, an), (sb, ap))):
            last = slice(which * n + n - OLD_B, which * n + n)
            edge = unpack(gright[last, :], gleft[last, :], 3)
            parts += [
                own[START_B:ROWS_A, :LANES] - other[START_B:ROWS_A, :],
                own[START_B:ROWS_A, LANES:] - edge,
            ]
        return parts

    def fresh(q):
        def make():
            here = slice(ROWS_A + q * half, ROWS_A + q * half + half)
            parts = []
            for own, new in ((sa, bn), (sb, bp)):
                both = new[ROWS_B:, :]
                right = pltpu.roll(both, 96, 1) if q else both
                left = both if q else pltpu.roll(both, 32, 1)
                edge = jnp.where(lane < 32, right, jnp.where(lane >= 96, left, 0.0))
                parts += [
                    own[here, :LANES] - new[q * half : q * half + half, :],
                    own[here, LANES:] - edge,
                ]
            return parts

        return (OLD_B + q * half, half, make)

    blocks = [(0, OLD_B, old), fresh(0), fresh(1)]
    base = START_B + HALO
    score_stage(
        WINDOWS_B,
        (1, 1, 2),
        blocks,
        flags,
        rh,
        rl,
        ch,
        cl,
        d,
        yh,
        yl,
        out,
        sem,
        (KEEP_A - base, COLS - base),
        base,
    )


def struct(*shape):
    return jax.ShapeDtypeStruct(shape, F32)


def cost(flops):
    return pl.CostEstimate(flops=flops, bytes_accessed=0, transcendentals=0)


def shards(image, offsets):
    x = image[0]
    position = lax.axis_index("bulk")
    side = lax.axis_index("swath")
    tiles = lax.axis_size("bulk")
    count = lax.axis_size("swath")
    toward = [(i, i + DIE_SPAN) for i in range(tiles - DIE_SPAN)]
    back = [(j, i) for i, j in toward]
    up = [(i, i + 1) for i in range(count - 1)]
    down = [(j, i) for i, j in up]
    flags = jnp.stack([position + DIE_SPAN < tiles, position >= DIE_SPAN, side > 0, side < count - 1]).astype(jnp.int32)
    rh, rl, ch, cl = pl.pallas_call(
        tables_kernel,
        out_shape=(
            jax.ShapeDtypeStruct((256, 512), BF16),
            jax.ShapeDtypeStruct((256, 256), BF16),
            jax.ShapeDtypeStruct((3, 4, WINDOW, 256), BF16),
            jax.ShapeDtypeStruct((3, 2, WINDOW, 256), BF16),
        ),
        in_specs=[SMEM],
        out_specs=(VMEM,) * 4,
        compiler_params=PARAMS,
        cost_estimate=cost(2_000_000_000),
        name="tables",
    )(flags)

    adn, aup, ny, pleft, pright = pl.pallas_call(
        head_kernel,
        out_shape=(
            struct(ROWS_A, LANES),
            struct(ROWS_A + 8, LANES),
            struct(8, LANES),
            struct(COLS // 4, LANES),
            struct(COLS // 4, LANES),
        ),
        in_specs=[SMEM, VMEM],
        out_specs=(VMEM,) * 5,
        compiler_params=PARAMS,
        name="head",
    )(offsets, x)
    an = lax.ppermute(adn, "bulk", back)
    ap = lax.ppermute(aup, "bulk", toward)
    from_right = lax.ppermute(pleft, "swath", down)
    from_left = lax.ppermute(pright, "swath", up)
    packed_b = ROWS_B + ROWS_B // 2
    h, bdn, bup = pl.pallas_call(
        edge_kernel,
        out_shape=(struct(COLS, LANES), struct(packed_b, LANES), struct(packed_b, LANES)),
        in_specs=[SMEM] + [VMEM] * 4,
        out_specs=(VMEM,) * 3,
        compiler_params=PARAMS,
        name="edge",
    )(offsets, x, ny, from_right, from_left)
    bn = lax.ppermute(bdn, "bulk", back)
    bp = lax.ppermute(bup, "bulk", toward)

    def shift(sign, move, spec):
        return pl.pallas_call(
            functools.partial(shift_kernel, sign),
            out_shape=struct(COLS, 2 * LANES),
            in_specs=[spec, VMEM, VMEM],
            out_specs=VMEM,
            scratch_shapes=[
                pltpu.VMEM((2, 256, COLS), BF16),
                pltpu.VMEM((2, 256, COLS), BF16),
                pltpu.VMEM((2, 1024, 256), BF16),
                pltpu.VMEM((2, 1024, 256), BF16),
            ],
            compiler_params=PARAMS,
            cost_estimate=cost(3_000_000_000),
            name="shift" + ("own" if sign > 0 else "back"),
        )(move, x, h)

    sa = shift(1, offsets, SMEM)
    quarter = ROWS_A // 2
    xleft, xright = pl.pallas_call(
        pack_kernel,
        out_shape=(struct(quarter, LANES), struct(quarter, LANES)),
        in_specs=[VMEM] * 2,
        out_specs=(VMEM,) * 2,
        compiler_params=PARAMS,
        name="pack",
    )(an, ap)
    gright = lax.ppermute(xleft, "swath", down)
    gleft = lax.ppermute(xright, "swath", up)
    sb = shift(-1, ap, VMEM)

    def scratch(count):
        length = count * WINDOW + 64
        return [
            pltpu.VMEM((length, 256), F32),
            pltpu.VMEM((4, length, 256), BF16),
            pltpu.VMEM((4, length, 256), BF16),
            pltpu.SemaphoreType.DMA,
        ]

    first = pl.pallas_call(
        first_kernel,
        out_shape=struct(COLS, LANES),
        in_specs=[SMEM] + [VMEM] * 10,
        out_specs=ANY,
        scratch_shapes=scratch(WINDOWS_A),
        compiler_params=PARAMS,
        cost_estimate=cost(3_000_000_000),
        name="first",
    )(flags, sa, sb, an, ap, gright, gleft, rh, rl, ch, cl)
    whole = pl.pallas_call(
        second_kernel,
        out_shape=struct(COLS, LANES),
        in_specs=[SMEM] + [VMEM] * 12 + [ANY],
        out_specs=ANY,
        scratch_shapes=scratch(WINDOWS_B),
        input_output_aliases={13: 0},
        compiler_params=PARAMS,
        name="second",
    )(flags, sa, sb, an, ap, gright, gleft, bn, bp, rh, rl, ch, cl, first)
    return whole[None]


def solution(mesh):
    return jax.shard_map(
        shards,
        mesh=mesh,
        in_specs=(P("bulk", None, "swath"), P("bulk")),
        out_specs=P("bulk", None, "swath"),
        check_vma=False,
    )
```

profile of v0, /device:TPU:80, one launch (start us, length us, event | category | flops | bytes accessed | tf_op | source)
XLA Modules:
  0.0 86.1 jit_solution(571574591372927898)
XLA Ops:
  0.7 0.0 copy-start
  0.7 1.2 %copy-done = f32[1,2048,128]{2,1,0:T(8,128)S(1)} copy-done((f32[1,2048,128]{2,1,0:T(8,128)S(1)}, f32[1,2048,128]{2,1,0:T(8,128)}, u32[]{:S(2)}) %copy-start) | copy-done | bytes 1048600
  1.9 1.2 %head.1 = (f32[1344,128]{1,0:T(8,128)S(1)}, f32[1352,128]{1,0:T(8,128)S(1)}, f32[8,128]{1,0:T(8,128)S(1)}, f32[512,128]{1,0:T(8,128)}, f32[512,128]{1,0:T(8,128)S(1)}) custom-call(s32[1]{0:T(128)S(6)} %copy.5.move, f32[2048,128]{1,0:T(8,128)S(1)} %bitcast.6), custom_call_target="tpu_custom_call" | custom-call | tf_op jit(solution)/shard_map/head/pallas_call | solution.py:394
  3.1 6.4 %collective-permute-start.2 = (f32[1352,128]{1,0:T(8,128)S(1)}, f32[1352,128]{1,0:T(8,128)S(1)}, u32[]{:S(2)}, u32[]{:S(2)}) collective-permute-start(f32[1352,128]{1,0:T(8,128)S(1)} %get-tuple-element.23), channel_id=1, source_target_pairs={{0,4},{1,5},{2,6},{3,7},{4,8},{5,9},{6,10},{7,11},{8,12},{9,13},{1... | collective-permute-start | bytes 2076680 | tf_op jit(solution)/shard_map/ppermute | solution.py:409
  9.5 1.9 %collective-permute-start.3 = (f32[1344,128]{1,0:T(8,128)S(1)}, f32[1344,128]{1,0:T(8,128)S(1)}, u32[]{:S(2)}, u32[]{:S(2)}) collective-permute-start(f32[1344,128]{1,0:T(8,128)S(1)} %get-tuple-element.24), channel_id=1, source_target_pairs={{4,0},{5,1},{6,2},{7,3},{8,4},{9,5},{10,6},{11,7},{12,8},{13,9},{1... | collective-permute-start | bytes 2064392 | tf_op jit(solution)/shard_map/ppermute | solution.py:408
  11.4 4.4 %collective-permute-start = (f32[512,128]{1,0:T(8,128)}, f32[512,128]{1,0:T(8,128)S(1)}, u32[]{:S(2)}, u32[]{:S(2)}) collective-permute-start(f32[512,128]{1,0:T(8,128)} %get-tuple-element.20), channel_id=1, source_target_pairs={{32,0},{64,32},{96,64},{128,96},{160,128},{192,160},{224,192},{33,... | collective-permute-start | bytes 786440 | tf_op jit(solution)/shard_map/ppermute | solution.py:410
  15.9 1.9 %collective-permute-start.1 = (f32[512,128]{1,0:T(8,128)S(1)}, f32[512,128]{1,0:T(8,128)S(1)}, u32[]{:S(2)}, u32[]{:S(2)}) collective-permute-start(f32[512,128]{1,0:T(8,128)S(1)} %get-tuple-element.21), channel_id=1, source_target_pairs={{0,32},{32,64},{64,96},{96,128},{128,160},{160,192},{192,224},{1,3... | collective-permute-start | bytes 786440 | tf_op jit(solution)/shard_map/ppermute | solution.py:411
  17.8 0.1 add_convert_fusion.flags
  17.9 0.0 copy-start.1
  17.9 3.5 %tables.1 = (bf16[256,512]{1,0:T(8,128)(2,1)S(1)}, bf16[256,256]{1,0:T(8,128)(2,1)S(1)}, bf16[3,4,192,256]{3,2,1,0:T(8,128)(2,1)S(1)}, bf16[3,2,192,256]{3,2,1,0:T(8,128)(2,1)S(1)}) custom-call(s32[4]{0:T(128)S(1)} %add_convert_fusion.flags), custom_call_target="tpu_custom_call" | custom-call | flops 2000000000 | tf_op jit(solution)/shard_map/tables/pallas_call | solution.py:379
  21.4 0.1 collective-permute-done.from_right
  21.4 7.4 %collective-permute-done.1.from_left = f32[512,128]{1,0:T(8,128)S(1)} collective-permute-done((f32[512,128]{1,0:T(8,128)S(1)}, f32[512,128]{1,0:T(8,128)S(1)}, u32[]{:S(2)}, u32[]{:S(2)}) %collective-permute-start.1) | collective-permute-done | bytes 262176 | tf_op jit(solution)/shard_map/ppermute | solution.py:411
  28.9 0.0 copy-done.1
  28.9 0.7 edge.1
  29.6 5.3 %collective-permute-start.6 = (f32[1056,128]{1,0:T(8,128)S(1)}, f32[1056,128]{1,0:T(8,128)S(1)}, u32[]{:S(2)}, u32[]{:S(2)}) collective-permute-start(f32[1056,128]{1,0:T(8,128)S(1)} %get-tuple-element.27), channel_id=1, source_target_pairs={{4,0},{5,1},{6,2},{7,3},{8,4},{9,5},{10,6},{11,7},{12,8},{13,9},{1... | collective-permute-start | bytes 1622024 | tf_op jit(solution)/shard_map/ppermute | solution.py:421
  34.9 2.6 %collective-permute-start.7 = (f32[1056,128]{1,0:T(8,128)S(1)}, f32[1056,128]{1,0:T(8,128)S(1)}, u32[]{:S(2)}, u32[]{:S(2)}) collective-permute-start(f32[1056,128]{1,0:T(8,128)S(1)} %get-tuple-element.28), channel_id=1, source_target_pairs={{0,4},{1,5},{2,6},{3,7},{4,8},{5,9},{6,10},{7,11},{8,12},{9,13},{1... | collective-permute-start | bytes 1622024 | tf_op jit(solution)/shard_map/ppermute | solution.py:422
  37.6 19.6 %collective-permute-done.3.an = f32[1344,128]{1,0:T(8,128)S(1)} collective-permute-done((f32[1344,128]{1,0:T(8,128)S(1)}, f32[1344,128]{1,0:T(8,128)S(1)}, u32[]{:S(2)}, u32[]{:S(2)}) %collective-permute-start.3) | collective-permute-done | bytes 688160 | tf_op jit(solution)/shard_map/ppermute | solution.py:408
  57.2 0.0 collective-permute-done.2.move.ap
  57.2 0.6 pack.1
  57.8 4.4 %collective-permute-start.4 = (f32[672,128]{1,0:T(8,128)S(1)}, f32[672,128]{1,0:T(8,128)S(1)}, u32[]{:S(2)}, u32[]{:S(2)}) collective-permute-start(f32[672,128]{1,0:T(8,128)S(1)} %get-tuple-element.25), channel_id=1, source_target_pairs={{32,0},{64,32},{96,64},{128,96},{160,128},{192,160},{224,192},{33,... | collective-permute-start | bytes 1032200 | tf_op jit(solution)/shard_map/ppermute | solution.py:451
  62.2 2.1 %collective-permute-start.5 = (f32[672,128]{1,0:T(8,128)S(1)}, f32[672,128]{1,0:T(8,128)S(1)}, u32[]{:S(2)}, u32[]{:S(2)}) collective-permute-start(f32[672,128]{1,0:T(8,128)S(1)} %get-tuple-element.26), channel_id=1, source_target_pairs={{0,32},{32,64},{64,96},{96,128},{128,160},{160,192},{192,224},{1,3... | collective-permute-start | bytes 1032200 | tf_op jit(solution)/shard_map/ppermute | solution.py:452
  64.3 4.1 %shiftown.1.sa = f32[2048,256]{1,0:T(8,128)S(1)} custom-call(s32[1]{0:T(128)S(6)} %copy.5.move, f32[2048,128]{1,0:T(8,128)S(1)} %bitcast.8, f32[2048,128]{1,0:T(8,128)S(1)} %get-tuple-element.22.h), custom_call_target="tpu_custom_call" | custom-call | flops 3000000000 | tf_op jit(solution)/shard_map/shiftown/pallas_call | solution.py:425
  68.5 4.1 %shiftback.1.sb = f32[2048,256]{1,0:T(8,128)S(1)} custom-call(f32[1352,128]{1,0:T(8,128)S(1)} %collective-permute-done.2.move.ap, f32[2048,128]{1,0:T(8,128)S(1)} %bitcast.9, f32[2048,128]{1,0:T(8,128)S(1)} %get-tuple-element.22.h), custom_call_target="tpu_custom_call" | custom-call | flops 3000000000 | tf_op jit(solution)/shard_map/shiftback/pallas_call | solution.py:425
  72.6 0.0 collective-permute-done.4.gright
  72.7 3.8 %collective-permute-done.5.gleft = f32[672,128]{1,0:T(8,128)S(1)} collective-permute-done((f32[672,128]{1,0:T(8,128)S(1)}, f32[672,128]{1,0:T(8,128)S(1)}, u32[]{:S(2)}, u32[]{:S(2)}) %collective-permute-start.5) | collective-permute-done | bytes 344096 | tf_op jit(solution)/shard_map/ppermute | solution.py:452
  76.4 5.6 %first.1._ = f32[2048,128]{1,0:T(8,128)} custom-call(s32[4]{0:T(128)S(1)} %add_convert_fusion.flags, f32[2048,256]{1,0:T(8,128)S(1)} %shiftown.1.sa, f32[2048,256]{1,0:T(8,128)S(1)} %shiftback.1.sb, f32[1344,128]{1,0:T(8,128)S(1)} %collective-permute-done.3.an, f32[1352,128]{1,0:T(8,128)S(1)} %collective-permute-done.2.move.ap, ...), custom_call_target="tpu_custom_call" | custom-call | flops 3000000000 | tf_op jit(solution)/shard_map/first/pallas_call | solution.py:464
  82.0 0.0 collective-permute-done.6.bn
  82.1 0.0 collective-permute-done.7.bp
  82.1 3.9 %second.1 = f32[2048,128]{1,0:T(8,128)} custom-call(s32[4]{0:T(128)S(1)} %add_convert_fusion.flags, f32[2048,256]{1,0:T(8,128)S(1)} %shiftown.1.sa, f32[2048,256]{1,0:T(8,128)S(1)} %shiftback.1.sb, f32[1344,128]{1,0:T(8,128)S(1)} %collective-permute-done.3.an, f32[1352,128]{1,0:T(8,128)S(1)} %collective-permute-done.2.move.ap, ...), custom_call_target="tpu_custom_call", output_to_operand_aliasing={{}: (13, {})} | custom-call | tf_op jit(solution)/shard_map/second/pallas_call | solution.py:474
Async XLA Ops:
  0.7 1.2 %copy-start = (f32[1,2048,128]{2,1,0:T(8,128)S(1)}, f32[1,2048,128]{2,1,0:T(8,128)}, u32[]{:S(2)}) copy-start(f32[1,2048,128]{2,1,0:T(8,128)} %param.2) | copy-start | bytes 3145732
  3.1 54.1 %collective-permute-start.2 = (f32[1352,128]{1,0:T(8,128)S(1)}, f32[1352,128]{1,0:T(8,128)S(1)}, u32[]{:S(2)}, u32[]{:S(2)}) collective-permute-start(f32[1352,128]{1,0:T(8,128)S(1)} %get-tuple-element.23), channel_id=1, source_target_pairs={{0,4},{1,5},{2,6},{3,7},{4,8},{5,9},{6,10},{7,11},{8,12},{9,13},{1... | collective-permute-start | bytes 2076680 | tf_op jit(solution)/shard_map/ppermute | solution.py:409
  9.5 47.7 %collective-permute-start.3 = (f32[1344,128]{1,0:T(8,128)S(1)}, f32[1344,128]{1,0:T(8,128)S(1)}, u32[]{:S(2)}, u32[]{:S(2)}) collective-permute-start(f32[1344,128]{1,0:T(8,128)S(1)} %get-tuple-element.24), channel_id=1, source_target_pairs={{4,0},{5,1},{6,2},{7,3},{8,4},{9,5},{10,6},{11,7},{12,8},{13,9},{1... | collective-permute-start | bytes 2064392 | tf_op jit(solution)/shard_map/ppermute | solution.py:408
  11.4 10.0 %collective-permute-start = (f32[512,128]{1,0:T(8,128)}, f32[512,128]{1,0:T(8,128)S(1)}, u32[]{:S(2)}, u32[]{:S(2)}) collective-permute-start(f32[512,128]{1,0:T(8,128)} %get-tuple-element.20), channel_id=1, source_target_pairs={{32,0},{64,32},{96,64},{128,96},{160,128},{192,160},{224,192},{33,... | collective-permute-start | bytes 786440 | tf_op jit(solution)/shard_map/ppermute | solution.py:410
  15.9 13.0 %collective-permute-start.1 = (f32[512,128]{1,0:T(8,128)S(1)}, f32[512,128]{1,0:T(8,128)S(1)}, u32[]{:S(2)}, u32[]{:S(2)}) collective-permute-start(f32[512,128]{1,0:T(8,128)S(1)} %get-tuple-element.21), channel_id=1, source_target_pairs={{0,32},{32,64},{64,96},{96,128},{128,160},{160,192},{192,224},{1,3... | collective-permute-start | bytes 786440 | tf_op jit(solution)/shard_map/ppermute | solution.py:411
  17.9 11.0 %copy-start.1 = (f32[1,2048,128]{2,1,0:T(8,128)S(1)}, f32[1,2048,128]{2,1,0:T(8,128)}, u32[]{:S(2)}) copy-start(f32[1,2048,128]{2,1,0:T(8,128)} %param.2) | copy-start | bytes 3145732
  29.6 52.5 %collective-permute-start.6 = (f32[1056,128]{1,0:T(8,128)S(1)}, f32[1056,128]{1,0:T(8,128)S(1)}, u32[]{:S(2)}, u32[]{:S(2)}) collective-permute-start(f32[1056,128]{1,0:T(8,128)S(1)} %get-tuple-element.27), channel_id=1, source_target_pairs={{4,0},{5,1},{6,2},{7,3},{8,4},{9,5},{10,6},{11,7},{12,8},{13,9},{1... | collective-permute-start | bytes 1622024 | tf_op jit(solution)/shard_map/ppermute | solution.py:421
  34.9 47.1 %collective-permute-start.7 = (f32[1056,128]{1,0:T(8,128)S(1)}, f32[1056,128]{1,0:T(8,128)S(1)}, u32[]{:S(2)}, u32[]{:S(2)}) collective-permute-start(f32[1056,128]{1,0:T(8,128)S(1)} %get-tuple-element.28), channel_id=1, source_target_pairs={{0,4},{1,5},{2,6},{3,7},{4,8},{5,9},{6,10},{7,11},{8,12},{9,13},{1... | collective-permute-start | bytes 1622024 | tf_op jit(solution)/shard_map/ppermute | solution.py:422
  57.8 14.9 %collective-permute-start.4 = (f32[672,128]{1,0:T(8,128)S(1)}, f32[672,128]{1,0:T(8,128)S(1)}, u32[]{:S(2)}, u32[]{:S(2)}) collective-permute-start(f32[672,128]{1,0:T(8,128)S(1)} %get-tuple-element.25), channel_id=1, source_target_pairs={{32,0},{64,32},{96,64},{128,96},{160,128},{192,160},{224,192},{33,... | collective-permute-start | bytes 1032200 | tf_op jit(solution)/shard_map/ppermute | solution.py:451
  62.2 14.2 %collective-permute-start.5 = (f32[672,128]{1,0:T(8,128)S(1)}, f32[672,128]{1,0:T(8,128)S(1)}, u32[]{:S(2)}, u32[]{:S(2)}) collective-permute-start(f32[672,128]{1,0:T(8,128)S(1)} %get-tuple-element.26), channel_id=1, source_target_pairs={{0,32},{32,64},{64,96},{96,128},{128,160},{160,192},{192,224},{1,3... | collective-permute-start | bytes 1032200 | tf_op jit(solution)/shard_map/ppermute | solution.py:452
where the time goes:
time: 86.9 us; the launch traced here: 86.1 us
  waiting for transfers between devices  30.9 us (36%)
  starting transfers between devices  29.1 us (33%)
  Pallas kernels  23.8 us (27%)
  local copies, waits for them, and re-layouts  1.22 us (1%)
  between operations  0.97 us (1%)
    ppermute x1, waiting for transfers between devices, shards(): an = lax.ppermute(adn, 'bulk', back)  19.6 us
    pallas_call x2, Pallas kernels, shift(): pl.pallas_call(functools.partial(shift_kernel, sign), out_shape=struct(CO...  8.28 us
    ppermute x1, waiting for transfers between devices, shards(): from_left = lax.ppermute(pright, 'swath', up)  7.41 us
    ppermute x1, starting transfers between devices, shards(): ap = lax.ppermute(aup, 'bulk', toward)  6.38 us
    pallas_call x1, Pallas kernels, shards(): pl.pallas_call(first_kernel, out_shape=struct(COLS, LANES), in_specs=[SME...  5.59 us
    ppermute x1, starting transfers between devices, shards(): bn = lax.ppermute(bdn, 'bulk', back)  5.34 us
    ppermute x1, starting transfers between devices, shards(): from_right = lax.ppermute(pleft, 'swath', down)  4.44 us
    ppermute x1, starting transfers between devices, shards(): gright = lax.ppermute(xleft, 'swath', down)  4.44 us
  transfers between devices with their start and end apart: 8, of which 4 were waited for; matrix products, arithmetic and copies ran while one was open for 0% of the time, Pallas kernels for 22%

commit v1 on v0

--- a/solution.py
+++ b/solution.py
@@ -12,7 +12,7 @@
 COLS = 2048
 LANES = 128
 HALO = 32
-ROWS_A = 1344
+ROWS_A = 1152
 ROWS_B = COLS - ROWS_A
 KEEP_A = ROWS_A - 32
 WINDOW = 192
@@ -228,7 +228,7 @@
     pack(ap[:ROWS_A, :], xleft, xright, ROWS_A // 4)
 
 
-def score_stage(count, cases, blocks, flags, row_high, row_low, col_high, col_low, d, yh, yl, out, sem, keep, base):
+def score_stage(count, cases, blocks, flags, row_high, row_low, col_high, col_low, d, yh, yl, emit):
     length = count * WINDOW + 64
     filled = []
     for start, rows, make in blocks:
@@ -261,7 +261,6 @@
             for k in range(4):
                 yh[k, low:high, :] = jnp.zeros((high - low, 256), BF16)
                 yl[k, low:high, :] = jnp.zeros((high - low, 256), BF16)
-    copies = []
     for w in range(count):
         case = cases[0] if w == 0 else cases[2] if w == count - 1 else cases[1]
         span = slice(WINDOW * w, WINDOW * w + 256)
@@ -275,16 +274,10 @@
             gap = before - after
             score = gap * gap if score is None else score + 2.0**k * (gap * gap)
             before = after
-        d[HALO + WINDOW * w : HALO + WINDOW * (w + 1), :LANES] = score[:, :LANES] * score[:, LANES:]
-    low, high = keep
-    copy = pltpu.make_async_copy(
-        d.at[pl.ds(HALO + low, high - low), pl.ds(0, LANES)], out.at[pl.ds(base + low, high - low)], sem
-    )
-    copy.start()
-    copy.wait()
-
-
-def first_kernel(flags, sa, sb, an, ap, gright, gleft, rh, rl, ch, cl, out, d, yh, yl, sem):
+        emit(w, score[:, :LANES] * score[:, LANES:])
+
+
+def first_kernel(flags, sa, sb, an, ap, gright, gleft, rh, rl, ch, cl, out, d, yh, yl):
     n = ROWS_A // 4
 
     def block(q):
@@ -298,12 +291,16 @@
 
         return (HALO + q * n, n, make)
 
-    score_stage(
-        WINDOWS_A, (0, 1, 1), [block(q) for q in range(4)], flags, rh, rl, ch, cl, d, yh, yl, out, sem, (0, KEEP_A), 0
-    )
-
-
-def second_kernel(flags, sa, sb, an, ap, gright, gleft, bn, bp, rh, rl, ch, cl, _, out, d, yh, yl, sem):
+    def emit(w, value):
+        out[WINDOW * w : WINDOW * (w + 1), :] = value
+
+    score_stage(WINDOWS_A, (0, 1, 1), [block(q) for q in range(4)], flags, rh, rl, ch, cl, d, yh, yl, emit)
+
+
+def second_kernel(flags, sa, sb, an, ap, gright, gleft, bn, bp, rh, rl, ch, cl, early, out, d, yh, yl, held, sem):
+    base = START_B + HALO
+    copies = [pltpu.make_async_copy(early.at[pl.ds(0, KEEP_A)], out.at[pl.ds(0, KEEP_A)], sem.at[WINDOWS_B])]
+    copies[0].start()
     n = ROWS_A // 4
     half = ROWS_B // 2
     lane = lanes((half, LANES))
@@ -337,24 +334,18 @@
         return (OLD_B + q * half, half, make)
 
     blocks = [(0, OLD_B, old), fresh(0), fresh(1)]
-    base = START_B + HALO
-    score_stage(
-        WINDOWS_B,
-        (1, 1, 2),
-        blocks,
-        flags,
-        rh,
-        rl,
-        ch,
-        cl,
-        d,
-        yh,
-        yl,
-        out,
-        sem,
-        (KEEP_A - base, COLS - base),
-        base,
-    )
+
+    def emit(w, value):
+        held[WINDOW * w : WINDOW * (w + 1), :] = value
+        low = max(WINDOW * w, KEEP_A - base)
+        count = WINDOW * (w + 1) - low
+        copy = pltpu.make_async_copy(held.at[pl.ds(low, count)], out.at[pl.ds(base + low, count)], sem.at[w])
+        copy.start()
+        copies.append(copy)
+
+    score_stage(WINDOWS_B, (1, 1, 2), blocks, flags, rh, rl, ch, cl, d, yh, yl, emit)
+    for copy in copies:
+        copy.wait()
 
 
 def struct(*shape):
@@ -418,8 +409,6 @@
         compiler_params=PARAMS,
         name="edge",
     )(offsets, x, ny, from_right, from_left)
-    bn = lax.ppermute(bdn, "bulk", back)
-    bp = lax.ppermute(bup, "bulk", toward)
 
     def shift(sign, move, spec):
         return pl.pallas_call(
@@ -439,6 +428,10 @@
         )(move, x, h)
 
     sa = shift(1, offsets, SMEM)
+    sa, bdn, bup = lax.optimization_barrier((sa, bdn, bup))
+    bn = lax.ppermute(bdn, "bulk", back)
+    bp = lax.ppermute(bup, "bulk", toward)
+    an, ap, sa = lax.optimization_barrier((an, ap, sa))
     quarter = ROWS_A // 2
     xleft, xright = pl.pallas_call(
         pack_kernel,
@@ -458,14 +451,13 @@
             pltpu.VMEM((length, 256), F32),
             pltpu.VMEM((4, length, 256), BF16),
             pltpu.VMEM((4, length, 256), BF16),
-            pltpu.SemaphoreType.DMA,
         ]
 
     first = pl.pallas_call(
         first_kernel,
-        out_shape=struct(COLS, LANES),
+        out_shape=struct(WINDOWS_A * WINDOW, LANES),
         in_specs=[SMEM] + [VMEM] * 10,
-        out_specs=ANY,
+        out_specs=VMEM,
         scratch_shapes=scratch(WINDOWS_A),
         compiler_params=PARAMS,
         cost_estimate=cost(3_000_000_000),
@@ -474,10 +466,10 @@
     whole = pl.pallas_call(
         second_kernel,
         out_shape=struct(COLS, LANES),
-        in_specs=[SMEM] + [VMEM] * 12 + [ANY],
+        in_specs=[SMEM] + [VMEM] * 13,
         out_specs=ANY,
-        scratch_shapes=scratch(WINDOWS_B),
-        input_output_aliases={13: 0},
+        scratch_shapes=scratch(WINDOWS_B)
+        + [pltpu.VMEM((WINDOWS_B * WINDOW, LANES), F32), pltpu.SemaphoreType.DMA((WINDOWS_B + 1,))],
         compiler_params=PARAMS,
         name="second",
     )(flags, sa, sb, an, ap, gright, gleft, bn, bp, rh, rl, ch, cl, first)

time: 86.9 us -> 83.1 us (0.956)
  waiting for transfers between devices: 30.9 us -> 27.7 us
  Pallas kernels: 23.8 us -> 22.3 us
  local copies, waits for them, and re-layouts: 1.22 us -> 2.45 us
    ppermute x1, waiting for transfers between devices: 19.6 us -> 13.3 us  [shards(): an = lax.ppermute(adn, 'bulk', back)]
    ppermute x1, waiting for transfers between devices: 0.06 us -> 3.24 us  [shards(): from_right = lax.ppermute(pleft, 'swath', down)]
    pallas_call x1, Pallas kernels: 5.59 us -> 4.29 us  [shards(): pl.pallas_call(first_kernel, out_shape=struct(WINDOWS_A * WINDOW, LANES),...]
    unnamed x4 -> x6, local copies, waits for them, and re-layouts: 1.22 us -> 2.45 us
  transfers between devices with their start and end apart: 8 -> 8, of which waited for: 4 -> 4; matrix products, arithmetic and copies ran while one was open for 0% -> 0% of each run, Pallas kernels for 22% -> 21%
where the time goes in v1:
time: 83.1 us; the launch traced here: 82.7 us
  starting transfers between devices  29.2 us (35%)
  waiting for transfers between devices  27.7 us (33%)
  Pallas kernels  22.3 us (27%)
  local copies, waits for them, and re-layouts  2.45 us (3%)
  between operations  0.99 us (1%)
    ppermute x1, waiting for transfers between devices, shards(): an = lax.ppermute(adn, 'bulk', back)  13.3 us
    pallas_call x2, Pallas kernels, shift(): pl.pallas_call(functools.partial(shift_kernel, sign), out_shape=struct(CO...  8.25 us
    ppermute x1, waiting for transfers between devices, shards(): from_left = lax.ppermute(pright, 'swath', up)  7.73 us
    ppermute x1, starting transfers between devices, shards(): ap = lax.ppermute(aup, 'bulk', toward)  6.39 us
    ppermute x1, starting transfers between devices, shards(): bn = lax.ppermute(bdn, 'bulk', back)  5.33 us
    pallas_call x1, Pallas kernels, shards(): pl.pallas_call(second_kernel, out_shape=struct(COLS, LANES), in_specs=[SM...  4.51 us
    ppermute x1, starting transfers between devices, shards(): from_right = lax.ppermute(pleft, 'swath', down)  4.44 us
    ppermute x1, starting transfers between devices, shards(): gright = lax.ppermute(xleft, 'swath', down)  4.3 us
  transfers between devices with their start and end apart: 8, of which 4 were waited for; matrix products, arithmetic and copies ran while one was open for 0% of the time, Pallas kernels for 21%

profile of v1, /device:TPU:80, one launch (start us, length us, event | category | flops | bytes accessed | tf_op | source)
XLA Modules:
  0.0 82.7 jit_solution(5806666778872508136)
XLA Ops:
  0.7 0.0 copy-start
  0.7 1.2 %copy-done = f32[1,2048,128]{2,1,0:T(8,128)S(1)} copy-done((f32[1,2048,128]{2,1,0:T(8,128)S(1)}, f32[1,2048,128]{2,1,0:T(8,128)}, u32[]{:S(2)}) %copy-start) | copy-done | bytes 1048600
  1.9 0.5 head.1
  2.4 6.4 %collective-permute-start.1 = (f32[1160,128]{1,0:T(8,128)S(1)}, f32[1160,128]{1,0:T(8,128)S(1)}, u32[]{:S(2)}, u32[]{:S(2)}) collective-permute-start(f32[1160,128]{1,0:T(8,128)S(1)} %get-tuple-element.26), channel_id=1, source_target_pairs={{0,4},{1,5},{2,6},{3,7},{4,8},{5,9},{6,10},{7,11},{8,12},{9,13},{1... | collective-permute-start | bytes 1781768 | tf_op jit(solution)/shard_map/ppermute | solution.py:400
  8.8 1.9 %collective-permute-start = (f32[1152,128]{1,0:T(8,128)S(1)}, f32[1152,128]{1,0:T(8,128)S(1)}, u32[]{:S(2)}, u32[]{:S(2)}) collective-permute-start(f32[1152,128]{1,0:T(8,128)S(1)} %get-tuple-element.25), channel_id=1, source_target_pairs={{4,0},{5,1},{6,2},{7,3},{8,4},{9,5},{10,6},{11,7},{12,8},{13,9},{1... | collective-permute-start | bytes 1769480 | tf_op jit(solution)/shard_map/ppermute | solution.py:399
  10.7 4.4 %collective-permute-start.2 = (f32[512,128]{1,0:T(8,128)S(1)}, f32[512,128]{1,0:T(8,128)S(1)}, u32[]{:S(2)}, u32[]{:S(2)}) collective-permute-start(f32[512,128]{1,0:T(8,128)S(1)} %get-tuple-element.28), channel_id=1, source_target_pairs={{32,0},{64,32},{96,64},{128,96},{160,128},{192,160},{224,192},{33,... | collective-permute-start | bytes 786440 | tf_op jit(solution)/shard_map/ppermute | solution.py:401
  15.2 1.9 %collective-permute-start.3 = (f32[512,128]{1,0:T(8,128)S(1)}, f32[512,128]{1,0:T(8,128)S(1)}, u32[]{:S(2)}, u32[]{:S(2)}) collective-permute-start(f32[512,128]{1,0:T(8,128)S(1)} %get-tuple-element.29), channel_id=1, source_target_pairs={{0,32},{32,64},{64,96},{96,128},{128,160},{160,192},{192,224},{1,3... | collective-permute-start | bytes 786440 | tf_op jit(solution)/shard_map/ppermute | solution.py:402
  17.1 0.1 add_convert_fusion.flags
  17.2 3.2 %collective-permute-done.2.from_right = f32[512,128]{1,0:T(8,128)S(1)} collective-permute-done((f32[512,128]{1,0:T(8,128)S(1)}, f32[512,128]{1,0:T(8,128)S(1)}, u32[]{:S(2)}, u32[]{:S(2)}) %collective-permute-start.2) | collective-permute-done | bytes 262176 | tf_op jit(solution)/shard_map/ppermute | solution.py:401
  20.4 7.7 %collective-permute-done.3.from_left = f32[512,128]{1,0:T(8,128)S(1)} collective-permute-done((f32[512,128]{1,0:T(8,128)S(1)}, f32[512,128]{1,0:T(8,128)S(1)}, u32[]{:S(2)}, u32[]{:S(2)}) %collective-permute-start.3) | collective-permute-done | bytes 262176 | tf_op jit(solution)/shard_map/ppermute | solution.py:402
  28.2 0.0 copy-start.1
  28.2 1.2 %copy-done.1 = f32[1,2048,128]{2,1,0:T(8,128)S(1)} copy-done((f32[1,2048,128]{2,1,0:T(8,128)S(1)}, f32[1,2048,128]{2,1,0:T(8,128)}, u32[]{:S(2)}) %copy-start.1) | copy-done | bytes 1048600
  29.4 0.8 edge.1
  30.2 4.1 %shiftown.1.sa = f32[2048,256]{1,0:T(8,128)S(1)} custom-call(s32[1]{0:T(128)S(6)} %copy.3.move, f32[2048,128]{1,0:T(8,128)S(1)} %bitcast.8, f32[2048,128]{1,0:T(8,128)S(1)} %get-tuple-element.30.h), custom_call_target="tpu_custom_call" | custom-call | flops 3000000000 | tf_op jit(solution)/shard_map/shiftown/pallas_call | solution.py:414
  34.3 5.3 %collective-permute-start.6 = (f32[1344,128]{1,0:T(8,128)S(1)}, f32[1344,128]{1,0:T(8,128)S(1)}, u32[]{:S(2)}, u32[]{:S(2)}) collective-permute-start(f32[1344,128]{1,0:T(8,128)S(1)} %get-tuple-element.39), channel_id=1, source_target_pairs={{4,0},{5,1},{6,2},{7,3},{8,4},{9,5},{10,6},{11,7},{12,8},{13,9},{1... | collective-permute-start | bytes 2064392 | tf_op jit(solution)/shard_map/ppermute | solution.py:432
  39.6 2.6 %collective-permute-start.7 = (f32[1344,128]{1,0:T(8,128)S(1)}, f32[1344,128]{1,0:T(8,128)S(1)}, u32[]{:S(2)}, u32[]{:S(2)}) collective-permute-start(f32[1344,128]{1,0:T(8,128)S(1)} %get-tuple-element.40), channel_id=1, source_target_pairs={{0,4},{1,5},{2,6},{3,7},{4,8},{5,9},{6,10},{7,11},{8,12},{9,13},{1... | collective-permute-start | bytes 2064392 | tf_op jit(solution)/shard_map/ppermute | solution.py:433
  42.3 13.3 %collective-permute-done.an = f32[1152,128]{1,0:T(8,128)S(1)} collective-permute-done((f32[1152,128]{1,0:T(8,128)S(1)}, f32[1152,128]{1,0:T(8,128)S(1)}, u32[]{:S(2)}, u32[]{:S(2)}) %collective-permute-start) | collective-permute-done | bytes 589856 | tf_op jit(solution)/shard_map/ppermute | solution.py:399
  55.6 0.0 collective-permute-done.1.move.ap
  55.6 0.5 pack.1
  56.1 4.3 %collective-permute-start.4 = (f32[576,128]{1,0:T(8,128)S(1)}, f32[576,128]{1,0:T(8,128)S(1)}, u32[]{:S(2)}, u32[]{:S(2)}) collective-permute-start(f32[576,128]{1,0:T(8,128)S(1)} %get-tuple-element.37), channel_id=1, source_target_pairs={{32,0},{64,32},{96,64},{128,96},{160,128},{192,160},{224,192},{33,... | collective-permute-start | bytes 884744 | tf_op jit(solution)/shard_map/ppermute | solution.py:444
  60.4 0.0 copy-start.2
  60.4 2.2 %collective-permute-start.5 = (f32[576,128]{1,0:T(8,128)S(1)}, f32[576,128]{1,0:T(8,128)S(1)}, u32[]{:S(2)}, u32[]{:S(2)}) collective-permute-start(f32[576,128]{1,0:T(8,128)S(1)} %get-tuple-element.38), channel_id=1, source_target_pairs={{0,32},{32,64},{64,96},{96,128},{128,160},{160,192},{192,224},{1,3... | collective-permute-start | bytes 884744 | tf_op jit(solution)/shard_map/ppermute | solution.py:445
  62.7 3.5 %tables.1 = (bf16[256,512]{1,0:T(8,128)(2,1)S(1)}, bf16[256,256]{1,0:T(8,128)(2,1)S(1)}, bf16[3,4,192,256]{3,2,1,0:T(8,128)(2,1)S(1)}, bf16[3,2,192,256]{3,2,1,0:T(8,128)(2,1)S(1)}) custom-call(s32[4]{0:T(128)S(1)} %add_convert_fusion.flags), custom_call_target="tpu_custom_call" | custom-call | flops 2000000000 | tf_op jit(solution)/shard_map/tables/pallas_call | solution.py:370
  66.1 0.0 copy-done.2
  66.2 4.1 %shiftback.1.sb = f32[2048,256]{1,0:T(8,128)S(1)} custom-call(f32[1160,128]{1,0:T(8,128)S(1)} %collective-permute-done.1.move.ap, f32[2048,128]{1,0:T(8,128)S(1)} %bitcast.9, f32[2048,128]{1,0:T(8,128)S(1)} %get-tuple-element.30.h), custom_call_target="tpu_custom_call" | custom-call | flops 3000000000 | tf_op jit(solution)/shard_map/shiftback/pallas_call | solution.py:414
  70.3 0.0 collective-permute-done.4.gright
  70.3 3.4 %collective-permute-done.5.gleft = f32[576,128]{1,0:T(8,128)S(1)} collective-permute-done((f32[576,128]{1,0:T(8,128)S(1)}, f32[576,128]{1,0:T(8,128)S(1)}, u32[]{:S(2)}, u32[]{:S(2)}) %collective-permute-start.5) | collective-permute-done | bytes 294944 | tf_op jit(solution)/shard_map/ppermute | solution.py:445
  73.7 4.3 %first.1.early = f32[1152,128]{1,0:T(8,128)S(1)} custom-call(s32[4]{0:T(128)S(1)} %add_convert_fusion.flags, f32[2048,256]{1,0:T(8,128)S(1)} %shiftown.1.sa, f32[2048,256]{1,0:T(8,128)S(1)} %shiftback.1.sb, f32[1152,128]{1,0:T(8,128)S(1)} %collective-permute-done.an, f32[1160,128]{1,0:T(8,128)S(1)} %collective-permute-done.1.move.ap, ...), custom_call_target="tpu_custom_call" | custom-call | flops 3000000000 | tf_op jit(solution)/shard_map/first/pallas_call | solution.py:456
  78.0 0.0 collective-permute-done.6.bn
  78.0 0.0 collective-permute-done.7.bp
  78.0 4.5 %second.1 = f32[2048,128]{1,0:T(8,128)} custom-call(s32[4]{0:T(128)S(1)} %add_convert_fusion.flags, f32[2048,256]{1,0:T(8,128)S(1)} %shiftown.1.sa, f32[2048,256]{1,0:T(8,128)S(1)} %shiftback.1.sb, f32[1152,128]{1,0:T(8,128)S(1)} %collective-permute-done.an, f32[1160,128]{1,0:T(8,128)S(1)} %collective-permute-done.1.move.ap, ...), custom_call_target="tpu_custom_call" | custom-call | tf_op jit(solution)/shard_map/second/pallas_call | solution.py:466
Async XLA Ops:
  0.7 1.2 %copy-start = (f32[1,2048,128]{2,1,0:T(8,128)S(1)}, f32[1,2048,128]{2,1,0:T(8,128)}, u32[]{:S(2)}) copy-start(f32[1,2048,128]{2,1,0:T(8,128)} %param.2) | copy-start | bytes 3145732
  2.4 53.2 %collective-permute-start.1 = (f32[1160,128]{1,0:T(8,128)S(1)}, f32[1160,128]{1,0:T(8,128)S(1)}, u32[]{:S(2)}, u32[]{:S(2)}) collective-permute-start(f32[1160,128]{1,0:T(8,128)S(1)} %get-tuple-element.26), channel_id=1, source_target_pairs={{0,4},{1,5},{2,6},{3,7},{4,8},{5,9},{6,10},{7,11},{8,12},{9,13},{1... | collective-permute-start | bytes 1781768 | tf_op jit(solution)/shard_map/ppermute | solution.py:400
  8.8 46.8 %collective-permute-start = (f32[1152,128]{1,0:T(8,128)S(1)}, f32[1152,128]{1,0:T(8,128)S(1)}, u32[]{:S(2)}, u32[]{:S(2)}) collective-permute-start(f32[1152,128]{1,0:T(8,128)S(1)} %get-tuple-element.25), channel_id=1, source_target_pairs={{4,0},{5,1},{6,2},{7,3},{8,4},{9,5},{10,6},{11,7},{12,8},{13,9},{1... | collective-permute-start | bytes 1769480 | tf_op jit(solution)/shard_map/ppermute | solution.py:399
  10.7 9.7 %collective-permute-start.2 = (f32[512,128]{1,0:T(8,128)S(1)}, f32[512,128]{1,0:T(8,128)S(1)}, u32[]{:S(2)}, u32[]{:S(2)}) collective-permute-start(f32[512,128]{1,0:T(8,128)S(1)} %get-tuple-element.28), channel_id=1, source_target_pairs={{32,0},{64,32},{96,64},{128,96},{160,128},{192,160},{224,192},{33,... | collective-permute-start | bytes 786440 | tf_op jit(solution)/shard_map/ppermute | solution.py:401
  15.2 13.0 %collective-permute-start.3 = (f32[512,128]{1,0:T(8,128)S(1)}, f32[512,128]{1,0:T(8,128)S(1)}, u32[]{:S(2)}, u32[]{:S(2)}) collective-permute-start(f32[512,128]{1,0:T(8,128)S(1)} %get-tuple-element.29), channel_id=1, source_target_pairs={{0,32},{32,64},{64,96},{96,128},{128,160},{160,192},{192,224},{1,3... | collective-permute-start | bytes 786440 | tf_op jit(solution)/shard_map/ppermute | solution.py:402
  28.2 1.2 %copy-start.1 = (f32[1,2048,128]{2,1,0:T(8,128)S(1)}, f32[1,2048,128]{2,1,0:T(8,128)}, u32[]{:S(2)}) copy-start(f32[1,2048,128]{2,1,0:T(8,128)} %param.2) | copy-start | bytes 3145732
  34.3 43.7 %collective-permute-start.6 = (f32[1344,128]{1,0:T(8,128)S(1)}, f32[1344,128]{1,0:T(8,128)S(1)}, u32[]{:S(2)}, u32[]{:S(2)}) collective-permute-start(f32[1344,128]{1,0:T(8,128)S(1)} %get-tuple-element.39), channel_id=1, source_target_pairs={{4,0},{5,1},{6,2},{7,3},{8,4},{9,5},{10,6},{11,7},{12,8},{13,9},{1... | collective-permute-start | bytes 2064392 | tf_op jit(solution)/shard_map/ppermute | solution.py:432
  39.6 38.4 %collective-permute-start.7 = (f32[1344,128]{1,0:T(8,128)S(1)}, f32[1344,128]{1,0:T(8,128)S(1)}, u32[]{:S(2)}, u32[]{:S(2)}) collective-permute-start(f32[1344,128]{1,0:T(8,128)S(1)} %get-tuple-element.40), channel_id=1, source_target_pairs={{0,4},{1,5},{2,6},{3,7},{4,8},{5,9},{6,10},{7,11},{8,12},{9,13},{1... | collective-permute-start | bytes 2064392 | tf_op jit(solution)/shard_map/ppermute | solution.py:433
  56.1 14.2 %collective-permute-start.4 = (f32[576,128]{1,0:T(8,128)S(1)}, f32[576,128]{1,0:T(8,128)S(1)}, u32[]{:S(2)}, u32[]{:S(2)}) collective-permute-start(f32[576,128]{1,0:T(8,128)S(1)} %get-tuple-element.37), channel_id=1, source_target_pairs={{32,0},{64,32},{96,64},{128,96},{160,128},{192,160},{224,192},{33,... | collective-permute-start | bytes 884744 | tf_op jit(solution)/shard_map/ppermute | solution.py:444
  60.4 5.8 %copy-start.2 = (f32[1,2048,128]{2,1,0:T(8,128)S(1)}, f32[1,2048,128]{2,1,0:T(8,128)}, u32[]{:S(2)}) copy-start(f32[1,2048,128]{2,1,0:T(8,128)} %param.2) | copy-start | bytes 3145732
  60.4 13.3 %collective-permute-start.5 = (f32[576,128]{1,0:T(8,128)S(1)}, f32[576,128]{1,0:T(8,128)S(1)}, u32[]{:S(2)}, u32[]{:S(2)}) collective-permute-start(f32[576,128]{1,0:T(8,128)S(1)} %get-tuple-element.38), channel_id=1, source_target_pairs={{0,32},{32,64},{64,96},{96,128},{128,160},{160,192},{192,224},{1,3... | collective-permute-start | bytes 884744 | tf_op jit(solution)/shard_map/ppermute | solution.py:445
